TPU v7x, 32 devices: a whole 2x2x4 slice. The times are simulated.
32 devices in a mesh: grp: 2 (over y), gy: 4 (over z), gx: 2 (over x), gz: 2 (over core).
Axes of the slice: x: 2, y: 2, z: 4, core: 2. Of those that a mesh axis runs over, the one named last changes fastest.
Arguments:
- pair: bfloat16 [1024, 512, 128], P(('grp', 'gx', 'gz'), 'gy'), parts along dimension 0, may hold values from -6 to 6
- lengths: int32 [2], P('grp'), parts along dimension 0, may hold values from 256 to 512
- ln_gain: float32 [128], replicated, may hold values from 0.1 to 1.9
- ln_bias: float32 [128], replicated, may hold values from -3 to 3
- w_ab: bfloat16 [128, 512], replicated, may hold values from -0.5 to 0.5
- w_gate: bfloat16 [128, 128], replicated, may hold values from -0.5 to 0.5
- out_gain: float32 [128], replicated, may hold values from 0.1 to 1.9
- out_bias: float32 [128], replicated, may hold values from -3 to 3
- w_out: bfloat16 [128, 128], replicated, may hold values from -0.5 to 0.5
Outputs:
- update: bfloat16 [1024, 512, 128], P(('grp', 'gx', 'gz'), 'gy'), parts along dimension 0
There are 2 independent parts, one for each index of `grp`. A program takes and returns all parts, laid end to end along the dimension named above; an argument that names none is the same for every part. Nothing has to cross between parts.
Inputs may be any that keep to these rules, and one draw needn't show every extreme that they name: Residues from lengths[0] on are padding.
All inputs are finite; a program needn't handle non-finite values.
Results may differ from a plain program's by a relative error of at most 0.0052.
Values may be sent and summed in bfloat16 or wider, within the bound.
A program may use at most 128 MiB of HBM per device.

v0:
```python
import jax
import jax.numpy as jnp
from jax import lax
from jax.sharding import PartitionSpec as P


def layer_norm(values, gain, bias):
    values = values.astype(jnp.float32)
    mean = jnp.mean(values, -1, keepdims=True)
    spread = jnp.mean(jnp.square(values - mean), -1, keepdims=True)
    return (values - mean) * lax.rsqrt(spread + 1e-05) * gain + bias


def channel_norm(values, gain, bias):
    mean = jnp.mean(values, 0, keepdims=True)
    spread = jnp.mean(jnp.square(values - mean), 0, keepdims=True)
    return (values - mean) * lax.rsqrt(spread + 1e-05) * gain[:, None, None] + bias[:, None, None]


def body(pair, lengths, ln_gain, ln_bias, w_ab, w_gate, out_gain, out_bias, w_out):
    tile_rows, tile_cols, width = pair.shape
    hidden = w_out.shape[0]
    row_start = lax.axis_index(("gx", "gz")) * tile_rows
    col_index = lax.axis_index("gy")
    col_start = col_index * tile_cols
    normed = layer_norm(pair, ln_gain, ln_bias).astype(jnp.bfloat16)
    flat = normed.reshape(tile_rows * tile_cols, width)
    proj = jnp.dot(flat, w_ab, preferred_element_type=jnp.float32).reshape(
        tile_rows, tile_cols, 4 * hidden
    )
    row_live = (row_start + jnp.arange(tile_rows, dtype=jnp.int32) < lengths[0]).astype(jnp.float32)
    col_live = (col_start + jnp.arange(tile_cols, dtype=jnp.int32) < lengths[0]).astype(jnp.float32)
    pair_mask = (row_live[:, None] * col_live[None, :])[..., None]
    left = (pair_mask * jax.nn.sigmoid(proj[..., :hidden]) * proj[..., hidden : 2 * hidden]).astype(
        jnp.bfloat16
    )
    right = (
        pair_mask * jax.nn.sigmoid(proj[..., 2 * hidden : 3 * hidden]) * proj[..., 3 * hidden :]
    ).astype(jnp.bfloat16)
    left_major = jnp.transpose(left, (2, 0, 1))
    right_major = jnp.transpose(right, (2, 0, 1))
    column_rows = lax.all_gather(right_major, ("gx", "gz"), axis=1, tiled=True)
    right_mine = lax.all_to_all(column_rows, "gy", split_axis=1, concat_axis=2, tiled=True)
    triangle = jnp.einsum(
        "cik,cjk->cij",
        lax.all_gather(left_major, "gy", axis=2, tiled=True),
        right_mine,
        preferred_element_type=jnp.float32,
    )
    tri_norm = channel_norm(triangle, out_gain, out_bias).astype(jnp.bfloat16)
    gate = jax.nn.sigmoid(jnp.dot(flat, w_gate, preferred_element_type=jnp.float32)).reshape(
        tile_rows, tile_cols, width
    )
    projected = jnp.einsum("cij,cd->ijd", tri_norm, w_out, preferred_element_type=jnp.float32)
    return (gate * projected).astype(jnp.bfloat16)


def solution(mesh):
    in_specs = (P(("grp", "gx", "gz"), "gy", None), P("grp"), P(), P(), P(), P(), P(), P(), P())
    out_specs = P(("grp", "gx", "gz"), "gy", None)
    return jax.shard_map(body, mesh=mesh, in_specs=in_specs, out_specs=out_specs, check_vma=False)
```

profile of v0, /device:TPU:9, one launch (start us, length us, event | category | flops | bytes accessed | tf_op | source)
XLA Modules:
  0.0 893.9 jit_solution(9406988459465322010)
XLA Ops:
  6.5 0.0 copy-start
  6.5 0.0 copy-start.7
  6.5 0.0 copy-start.6
  6.5 0.0 all-gather.5.cloned.1.call-start
  6.6 0.0 copy-start.3
  7.4 3.8 convert_reduce_fusion
  11.2 6.0 fusion.5
  17.2 0.1 broadcast_multiply_fusion
  17.3 0.0 copy-done.7
  17.3 0.0 copy-done.6
  17.3 0.0 copy-done.3
  17.4 4.9 fusion.8
  22.3 0.0 copy-done
  22.3 0.0 copy-start.4
  22.3 13.2 %fusion.25 = f32[128,128,512]{2,1,0:T(8,128)} fusion(bf16[128,128,128]{2,1,0:T(8,128)(2,1)S(1)} %fusion.8, bf16[128,512]{1,0:T(8,128)(2,1)S(1)} %copy-done), kind=kOutput, calls=%fused_computation.34 | convolution fusion | flops 2147483648 | bytes 37879808 | tf_op jit(solution)/shard_map/dot_general | solution.py:28
  35.5 0.0 copy-done.4
  35.5 15.6 %fusion.22 = (bf16[128,128,128]{0,2,1:T(8,128)(2,1)}, bf16[128,128,128]{0,2,1:T(8,128)(2,1)}) fusion(f32[128,128,512]{2,1,0:T(8,128)} %fusion.25, f32[128,128]{1,0:T(8,128)S(1)} %broadcast_multiply_fusion), kind=kLoop, calls=%fused_computation.33 | loop fusion | flops 25165824 | bytes 42008576 | tf_op jit(solution)/shard_map/transpose | solution.py:41
  51.1 6.4 copy.13
  57.4 0.0 all-gather.5.cloned.1.call-update
  57.5 0.0 all-gather.3.cloned.1.call-start
  57.5 0.7 all-gather.3.cloned.1.call-update
  58.2 0.0 copy-start.10
  58.2 106.8 %all-gather.5.cloned.1.call-done = bf16[128,512,128]{2,0,1:T(8,128)(2,1)} async-done(((bf16[128,128,128]{2,0,1:T(8,128)(2,1)}), bf16[128,512,128]{2,0,1:T(8,128)(2,1)}) %all-gather.5.cloned.1.call-update) | async-done | bytes 16777232 | tf_op jit(solution)/shard_map/all_gather | solution.py:42
  165.1 7.3 all-to-all-start
  172.4 0.0 copy-done.10
  172.4 9.1 %fusion.2 = f32[16384,128]{1,0:T(8,128)} fusion(bf16[16384,128]{1,0:T(8,128)(2,1)} %bitcast.24, bf16[128,128]{1,0:T(8,128)(2,1)S(1)} %copy-done.10), kind=kOutput, calls=%fused_computation.3 | convolution fusion | flops 543162368 | bytes 12615680 | tf_op jit(solution)/shard_map/dot_general | solution.py:51
  181.4 583.0 %all-gather.3.cloned.1.call-done = bf16[128,128,512]{0,2,1:T(8,128)(2,1)} async-done(((bf16[128,128,128]{0,2,1:T(8,128)(2,1)}), bf16[128,128,512]{0,2,1:T(8,128)(2,1)}) %all-gather.3.cloned.1.call-update) | async-done | bytes 16777232 | tf_op jit(solution)/shard_map/all_gather | solution.py:46
  764.5 23.4 %copy.15 = bf16[128,128,512]{2,1,0:T(8,128)(2,1)} copy(bf16[128,128,512]{0,2,1:T(8,128)(2,1)} %all-gather.3.cloned.1.call-done) | data formatting | bytes 33554432 | tf_op jit(solution)/shard_map/all_gather | solution.py:46
  787.9 13.8 %all-to-all-done = bf16[128,512,128]{2,0,1:T(8,128)(2,1)} async-done(((bf16[128,512,128]{2,0,1:T(8,128)(2,1)}), bf16[128,512,128]{2,0,1:T(8,128)(2,1)}, u32[]{:S(2)}, u32[]{:S(2)}) %all-to-all-start) | async-done | bytes 16777248 | tf_op jit(solution)/shard_map/all_to_all | solution.py:43
  801.7 22.0 %copy.22 = bf16[128,4,128,128]{3,1,2,0:T(4,128)(2,1)} copy(bf16[128,4,128,128]{3,0,2,1:T(8,128)(2,1)} %bitcast.6) | data formatting | bytes 33554432 | tf_op jit(solution)/shard_map/all_to_all | solution.py:43
  823.7 24.9 %all_to_all.16 = bf16[128,128,512]{2,1,0:T(8,128)(2,1)} reshape(bf16[128,128,4,128]{3,2,1,0:T(4,128)(2,1)} %bitcast.23) | data formatting | bytes 33554432 | tf_op jit(solution)/shard_map/all_to_all | solution.py:43
  848.6 16.4 %fusion.28 = (f32[128,128]{1,0:T(8,128)S(1)}, f32[128,128,128]{2,1,0:T(8,128)}) fusion(bf16[128,128,512]{2,1,0:T(8,128)(2,1)} %copy.15, bf16[128,128,512]{2,1,0:T(8,128)(2,1)} %all_to_all.16), kind=kOutput, calls=%fused_computation.44 | convolution fusion | flops 2149564416 | bytes 42008576 | tf_op jit(solution)/shard_map/cik,cjk->cij/dot_general | solution.py:44
  865.0 0.0 copy-start.2
  865.0 0.0 copy-start.8
  865.0 0.0 copy-start.9
  865.0 4.4 multiply_reduce_fusion
  869.4 0.0 copy-start.5
  869.4 1.3 copy-done.2
  870.7 0.0 copy-done.8
  870.7 0.0 copy-done.9
  870.7 2.0 add_convert_fusion
  872.7 0.0 copy-start.1
  872.7 0.0 copy-done.5
  872.7 14.4 %multiply_convert_fusion = bf16[128,128,128]{2,1,0:T(8,128)(2,1)} fusion(f32[128,128,128]{2,1,0:T(8,128)} %bitcast.25, bf16[128,128,128]{2,1,0:T(8,128)(2,1)S(1)} %add_convert_fusion, bf16[128,128]{1,0:T(8,128)(2,1)S(1)} %copy-done.5), kind=kOutput, calls=%fused_computation.27 | convolution fusion | flops 541065216 | bytes 16809984 | tf_op jit(solution)/shard_map/cij,cd->ijd/dot_general | solution.py:54
  887.1 0.0 copy-done.1
  (5 shorter events, 0.1 us)
Async XLA Ops:
  6.5 15.8 %copy-start = (bf16[128,512]{1,0:T(8,128)(2,1)S(1)}, bf16[128,512]{1,0:T(8,128)(2,1)}, u32[]{:S(2)}) copy-start(bf16[128,512]{1,0:T(8,128)(2,1)} %param.13) | copy-start | bytes 393220
  6.5 10.8 %copy-start.7 = (f32[128]{0:T(128)S(1)}, f32[128]{0:T(128)}, u32[]{:S(2)}) copy-start(f32[128]{0:T(128)} %param.11) | copy-start | bytes 1540
  6.5 10.8 %copy-start.6 = (f32[128]{0:T(128)S(1)}, f32[128]{0:T(128)}, u32[]{:S(2)}) copy-start(f32[128]{0:T(128)} %param.12) | copy-start | bytes 1540
  6.5 158.5 %all-gather.5.cloned.1.call-start = ((), (), s32[]{:S(2)}) async-start(), calls=%async_computation.2 | async-start | bytes 20971520 | tf_op jit(solution)/shard_map/all_gather | solution.py:42
  6.6 10.8 %copy-start.3 = (bf16[128,128,128]{2,1,0:T(8,128)(2,1)S(1)}, bf16[128,128,128]{2,1,0:T(8,128)(2,1)}, u32[]{:S(2)}) copy-start(bf16[128,128,128]{2,1,0:T(8,128)(2,1)} %param.9) | copy-start | bytes 12582916
  22.3 13.2 %copy-start.4 = (bf16[128,128,128]{2,1,0:T(8,128)(2,1)}, bf16[128,128,128]{2,1,0:T(8,128)(2,1)S(1)}, u32[]{:S(2)}) copy-start(bf16[128,128,128]{2,1,0:T(8,128)(2,1)S(1)} %fusion.8) | copy-start | bytes 12582916
  57.5 707.0 %all-gather.3.cloned.1.call-start = ((), (), s32[]{:S(2)}) async-start(), calls=%async_computation.1 | async-start | bytes 20971520 | tf_op jit(solution)/shard_map/all_gather | solution.py:46
  58.2 114.2 %copy-start.10 = (bf16[128,128]{1,0:T(8,128)(2,1)S(1)}, bf16[128,128]{1,0:T(8,128)(2,1)}, u32[]{:S(2)}) copy-start(bf16[128,128]{1,0:T(8,128)(2,1)} %param.14) | copy-start | bytes 98308
  165.1 636.6 %all-to-all-start = ((bf16[128,512,128]{2,0,1:T(8,128)(2,1)}), bf16[128,512,128]{2,0,1:T(8,128)(2,1)}, u32[]{:S(2)}, u32[]{:S(2)}) async-start(bf16[128,512,128]{2,0,1:T(8,128)(2,1)} %all-gather.5.cloned.1.call-done), calls=%async_computation | async-start | bytes 33554432 | tf_op jit(solution)/shard_map/all_to_all | solution.py:43
  865.0 5.8 copy-start.2
  865.0 5.8 copy-start.8
  865.0 5.8 copy-start.9
  869.4 3.3 copy-start.5
  872.7 14.4 %copy-start.1 = (bf16[128,512]{1,0:T(8,128)(2,1)S(1)}, bf16[128,512]{1,0:T(8,128)(2,1)}, u32[]{:S(2)}) copy-start(bf16[128,512]{1,0:T(8,128)(2,1)} %param.13) | copy-start | bytes 393220
Sparse Core Ops, SparseCore 0:
  57.6 107.4 all-gather.4
  166.6 597.7 all-gather.2
where the time goes:
time: 900 us; the launch traced here: 894 us
  waiting for transfers between devices  704 us (78%)
  local copies, waits for them, and re-layouts  78 us (9%)
  matrix products  52.9 us (6%)
  other arithmetic  36.9 us (4%)
  between operations  14.4 us (2%)
    all_gather x1, waiting for transfers between devices, body(): lax.all_gather(left_major, 'gy', axis=2, tiled=True)  583 us
    all_gather x1, waiting for transfers between devices, body(): column_rows = lax.all_gather(right_major, ('gx', 'gz'), axis=1, tiled=True)  107 us
    all_to_all x2, local copies, waits for them, and re-layouts, body(): lax.all_to_all(column_rows, 'gy', split_axis=1, concat_axis=2, tiled=True)  46.9 us
    all_gather x1, local copies, waits for them, and re-layouts, body(): lax.all_gather(left_major, 'gy', axis=2, tiled=True)  23.4 us
  transfers between devices with their start and end apart: 3, of which 3 were waited for; matrix products, arithmetic and copies ran while one was open for 4% of the time, Pallas kernels for 0%

commit v1 on v0

--- a/solution.py
+++ b/solution.py
@@ -1,7 +1,14 @@
+import functools
+
 import jax
 import jax.numpy as jnp
 from jax import lax
+from jax.experimental import pallas as pl
+from jax.experimental.pallas import tpu as pltpu
 from jax.sharding import PartitionSpec as P
+
+CHUNKS = 2
+ROWS = 16
 
 
 def layer_norm(values, gain, bias):
@@ -17,7 +24,7 @@
     return (values - mean) * lax.rsqrt(spread + 1e-05) * gain[:, None, None] + bias[:, None, None]
 
 
-def body(pair, lengths, ln_gain, ln_bias, w_ab, w_gate, out_gain, out_bias, w_out):
+def gather_body(pair, lengths, ln_gain, ln_bias, w_ab, w_gate, out_gain, out_bias, w_out):
     tile_rows, tile_cols, width = pair.shape
     hidden = w_out.shape[0]
     row_start = lax.axis_index(("gx", "gz")) * tile_rows
@@ -55,7 +62,233 @@
     return (gate * projected).astype(jnp.bfloat16)
 
 
+def project_kernel(lengths, starts, pair, gain, bias, w_t, out):
+    rows, cols, width = pair.shape
+    hidden = out.shape[1]
+    flat = pair[...].reshape(rows * cols, width)
+    normed = layer_norm(flat, gain[...], bias[...]).astype(jnp.bfloat16)
+    proj = lax.dot_general(
+        w_t[...], normed, (((1,), (1,)), ((), ())), preferred_element_type=jnp.float32
+    )
+    lane = lax.broadcasted_iota(jnp.int32, (1, rows * cols), 1)
+    row = starts[0] + pl.program_id(0) * rows + lane // cols
+    col = starts[1] + lane % cols
+    mask = ((row < lengths[0]) & (col < lengths[0])).astype(jnp.float32)
+    for side in range(2):
+        base = 2 * side * hidden
+        value = (
+            mask * jax.nn.sigmoid(proj[base : base + hidden]) * proj[base + hidden : base + 2 * hidden]
+        )
+        out[side] = value.reshape(hidden, rows, cols).astype(jnp.bfloat16)
+
+
+def exchange_kernel(
+    ny, nx, nz, send, out, held, tri, in_send, in_recv, out_send, out_recv, own_sem
+):
+    n = ny * nx * nz
+    hidden, rows, cols = send.shape[1:]
+    each = hidden // n
+    part = each // CHUNKS
+    gy, gx, gz = lax.axis_index("gy"), lax.axis_index("gx"), lax.axis_index("gz")
+    me = (gx * nz + gz) * ny + gy
+
+    def where(index):
+        tall, wide = index // ny, index % ny
+        return (
+            {"gy": wide, "gx": tall // nz, "gz": tall % nz},
+            pl.ds(pl.multiple_of(tall * rows, rows), rows),
+            pl.ds(pl.multiple_of(wide * cols, cols), cols),
+        )
+
+    def deal(chunk, step):
+        peer = lax.rem(me + step, n)
+        _, my_rows, my_cols = where(me)
+        slot = chunk * n + step
+        return pltpu.make_async_remote_copy(
+            src_ref=send.at[:, pl.ds(peer * each + chunk * part, part)],
+            dst_ref=held.at[:, pl.ds(chunk * part, part), my_rows, my_cols],
+            send_sem=in_send.at[slot],
+            recv_sem=in_recv.at[slot],
+            device_id=where(peer)[0],
+            device_id_type=pl.DeviceIdType.MESH,
+        )
+
+    def hand_back(chunk, step):
+        peer = lax.rem(me + step, n)
+        device, its_rows, its_cols = where(peer)
+        slot = chunk * n + step
+        return pltpu.make_async_remote_copy(
+            src_ref=tri.at[pl.ds(chunk * part, part), its_rows, its_cols],
+            dst_ref=out.at[pl.ds(me * each + chunk * part, part)],
+            send_sem=out_send.at[slot],
+            recv_sem=out_recv.at[slot],
+            device_id=device,
+            device_id_type=pl.DeviceIdType.MESH,
+        )
+
+    def keep_in(chunk):
+        _, my_rows, my_cols = where(me)
+        return pltpu.make_async_copy(
+            send.at[:, pl.ds(me * each + chunk * part, part)],
+            held.at[:, pl.ds(chunk * part, part), my_rows, my_cols],
+            own_sem.at[chunk],
+        )
+
+    def keep_out(chunk):
+        _, my_rows, my_cols = where(me)
+        return pltpu.make_async_copy(
+            tri.at[pl.ds(chunk * part, part), my_rows, my_cols],
+            out.at[pl.ds(me * each + chunk * part, part)],
+            own_sem.at[CHUNKS + chunk],
+        )
+
+    barrier = pltpu.get_barrier_semaphore()
+    for step in range(1, n):
+        pl.semaphore_signal(
+            barrier,
+            inc=1,
+            device_id=where(lax.rem(me + step, n))[0],
+            device_id_type=pl.DeviceIdType.MESH,
+        )
+    pl.semaphore_wait(barrier, n - 1)
+
+    for chunk in range(CHUNKS):
+        for step in range(1, n):
+            deal(chunk, step).start()
+        keep_in(chunk).start()
+    for chunk in range(CHUNKS):
+        for step in range(1, n):
+            deal(chunk, step).wait_recv()
+        keep_in(chunk).wait()
+
+        @pl.loop(chunk * part, (chunk + 1) * part)
+        def _(channel):
+            tri[channel] = lax.dot_general(
+                held[0, channel],
+                held[1, channel],
+                (((1,), (1,)), ((), ())),
+                preferred_element_type=jnp.float32,
+            ).astype(jnp.bfloat16)
+
+        for step in range(1, n):
+            hand_back(chunk, step).start()
+        keep_out(chunk).start()
+    for chunk in range(CHUNKS):
+        for step in range(1, n):
+            hand_back(chunk, step).wait_recv()
+            deal(chunk, step).wait_send()
+            hand_back(chunk, step).wait_send()
+        keep_out(chunk).wait()
+
+
+def finish_kernel(pair, tri, gain, bias, w_gate, out_gain, out_bias, w_out, out):
+    rows, cols, width = pair.shape
+    hidden = tri.shape[0]
+    flat = pair[...].reshape(rows * cols, width)
+    normed = layer_norm(flat, gain[...], bias[...]).astype(jnp.bfloat16)
+    gate = jax.nn.sigmoid(jnp.dot(normed, w_gate[...], preferred_element_type=jnp.float32))
+    values = tri[...].astype(jnp.float32)
+    mean = jnp.mean(values, 0, keepdims=True)
+    centred = values - mean
+    spread = jnp.mean(jnp.square(centred), 0, keepdims=True)
+    scaled = (centred * lax.rsqrt(spread + 1e-05)).reshape(hidden, rows * cols)
+    tri_norm = (scaled * out_gain[...] + out_bias[...]).astype(jnp.bfloat16)
+    projected = lax.dot_general(
+        tri_norm, w_out[...], (((0,), (0,)), ((), ())), preferred_element_type=jnp.float32
+    )
+    out[...] = (gate * projected).astype(jnp.bfloat16).reshape(rows, cols, width)
+
+
+def whole(shape):
+    return pl.BlockSpec(shape, lambda step: (0,) * len(shape))
+
+
+def channel_body(sizes, pair, lengths, ln_gain, ln_bias, w_ab, w_gate, out_gain, out_bias, w_out):
+    ny, nx, nz = sizes
+    n = ny * nx * nz
+    tile_rows, tile_cols, width = pair.shape
+    hidden = w_out.shape[0]
+    starts = jnp.stack(
+        [lax.axis_index(("gx", "gz")) * tile_rows, lax.axis_index("gy") * tile_cols]
+    ).astype(jnp.int32)
+    gain, bias = ln_gain[None, :], ln_bias[None, :]
+    smem = pl.BlockSpec(memory_space=pltpu.SMEM)
+    steps = tile_rows // ROWS
+    sides = pl.pallas_call(
+        project_kernel,
+        name="project",
+        grid=(steps,),
+        out_shape=jax.ShapeDtypeStruct((2, hidden, tile_rows, tile_cols), jnp.bfloat16),
+        in_specs=[
+            smem,
+            smem,
+            pl.BlockSpec((ROWS, tile_cols, width), lambda step: (step, 0, 0)),
+            whole((1, width)),
+            whole((1, width)),
+            whole((4 * hidden, width)),
+        ],
+        out_specs=pl.BlockSpec((2, hidden, ROWS, tile_cols), lambda step: (0, 0, step, 0)),
+        compiler_params=pltpu.CompilerParams(vmem_limit_bytes=56 * 2**20),
+    )(lengths, starts, pair, gain, bias, w_ab.T)
+    dma = pltpu.SemaphoreType.DMA
+    any_space = pl.BlockSpec(memory_space=pl.ANY)
+    triangle = pl.pallas_call(
+        functools.partial(exchange_kernel, ny, nx, nz),
+        name="exchange",
+        out_shape=jax.ShapeDtypeStruct((hidden, tile_rows, tile_cols), jnp.bfloat16),
+        in_specs=[any_space],
+        out_specs=any_space,
+        scratch_shapes=[
+            pltpu.VMEM((2, hidden // n, nx * nz * tile_rows, ny * tile_cols), jnp.bfloat16),
+            pltpu.VMEM((hidden // n, nx * nz * tile_rows, ny * tile_cols), jnp.bfloat16),
+            dma((CHUNKS * n,)),
+            dma((CHUNKS * n,)),
+            dma((CHUNKS * n,)),
+            dma((CHUNKS * n,)),
+            dma((2 * CHUNKS,)),
+        ],
+        compiler_params=pltpu.CompilerParams(
+            collective_id=0, has_side_effects=True, vmem_limit_bytes=48 * 2**20
+        ),
+    )(sides)
+    return pl.pallas_call(
+        finish_kernel,
+        name="finish",
+        grid=(steps,),
+        out_shape=jax.ShapeDtypeStruct(pair.shape, jnp.bfloat16),
+        in_specs=[
+            pl.BlockSpec((ROWS, tile_cols, width), lambda step: (step, 0, 0)),
+            pl.BlockSpec((hidden, ROWS, tile_cols), lambda step: (0, step, 0)),
+            whole((1, width)),
+            whole((1, width)),
+            whole((width, width)),
+            whole((hidden, 1)),
+            whole((hidden, 1)),
+            whole((hidden, width)),
+        ],
+        out_specs=pl.BlockSpec((ROWS, tile_cols, width), lambda step: (step, 0, 0)),
+        compiler_params=pltpu.CompilerParams(vmem_limit_bytes=56 * 2**20),
+    )(pair, triangle, gain, bias, w_gate, out_gain[:, None], out_bias[:, None], w_out)
+
+
+def body(sizes, pair, *rest):
+    ny, nx, nz = sizes
+    n = ny * nx * nz
+    hidden = rest[-1].shape[0]
+    tile_rows, tile_cols, _ = pair.shape
+    fits = (
+        hidden % (n * CHUNKS) == 0
+        and tile_rows == tile_cols
+        and ny == nx * nz
+        and tile_cols % 128 == 0
+    )
+    return channel_body(sizes, pair, *rest) if fits else gather_body(pair, *rest)
+
+
 def solution(mesh):
     in_specs = (P(("grp", "gx", "gz"), "gy", None), P("grp"), P(), P(), P(), P(), P(), P(), P())
     out_specs = P(("grp", "gx", "gz"), "gy", None)
-    return jax.shard_map(body, mesh=mesh, in_specs=in_specs, out_specs=out_specs, check_vma=False)
+    sizes = (mesh.shape["gy"], mesh.shape["gx"], mesh.shape["gz"])
+    return jax.shard_map(
+        functools.partial(body, sizes), mesh=mesh, in_specs=in_specs, out_specs=out_specs, check_vma=False
+    )

time: 900 us -> 313 us (0.35)
  waiting for transfers between devices: 704 us -> 0 us
  Pallas kernels: 0 us -> 306 us
  local copies, waits for them, and re-layouts: 78 us -> 5.06 us
  matrix products: 52.9 us -> 0 us
  other arithmetic: 36.9 us -> 0.59 us
  between operations: 14.4 us -> 0.67 us
    all_gather x2 -> x0, waiting for transfers between devices: 690 us -> none  [the longest x1 583 us: body(): lax.all_gather(left_major, 'gy', axis=2, tiled=True)]
    pallas_call x0 -> x3, Pallas kernels: none -> 306 us  [the longest x1 278 us: channel_body(): pl.pallas_call(functools.partial(exchange_kernel, ny, nx, nz), name='exch...]
    dot_general x4 -> x0, matrix products: 52.9 us -> none  [the longest x1 16.4 us: body(): jnp.einsum('cik,cjk->cij', lax.all_gather(left_major, 'gy', axis=2, tiled...]
    all_to_all x2 -> x0, local copies, waits for them, and re-layouts: 46.9 us -> none  [body(): lax.all_to_all(column_rows, 'gy', split_axis=1, concat_axis=2, tiled=True)]
    all_gather x1 -> x0, local copies, waits for them, and re-layouts: 23.4 us -> none  [body(): lax.all_gather(left_major, 'gy', axis=2, tiled=True)]
    transpose x1 -> x0, other arithmetic: 15.6 us -> none  [body(): right_major = jnp.transpose(right, (2, 0, 1))]
    reduce_sum x3 -> x0, other arithmetic: 14.2 us -> none  [the longest x1 5.99 us: layer_norm(): spread = jnp.mean(jnp.square(values - mean), -1, keepdims=True)]
    all_to_all x1 -> x0, waiting for transfers between devices: 13.8 us -> none  [body(): lax.all_to_all(column_rows, 'gy', split_axis=1, concat_axis=2, tiled=True)]
  transfers between devices with their start and end apart: 3 -> 0, of which waited for: 3 -> 0; matrix products, arithmetic and copies ran while one was open for 4% -> 0% of each run, Pallas kernels for 0% -> 0%
where the time goes in v1:
time: 313 us; the launch traced here: 312 us
  Pallas kernels  306 us (98%)
  local copies, waits for them, and re-layouts  5.06 us (2%)
    pallas_call x1, Pallas kernels, channel_body(): pl.pallas_call(functools.partial(exchange_kernel, ny, nx, nz), name='exch...  278 us
    pallas_call x1, Pallas kernels, channel_body(): pl.pallas_call(project_kernel, name='project', grid=(steps,), out_shape=j...  14 us
    pallas_call x1, Pallas kernels, channel_body(): pl.pallas_call(finish_kernel, name='finish', grid=(steps,), out_shape=jax...  13.8 us

profile of v1, /device:TPU:9, one launch (start us, length us, event | category | flops | bytes accessed | tf_op | source)
XLA Modules:
  0.0 312.3 jit_solution(16378378837111631481)
XLA Ops:
  0.0 0.6 pad_add_fusion.starts
  0.6 1.7 copy.10
  2.9 14.0 %project.1.send = bf16[2,128,128,128]{3,2,1,0:T(8,128)(2,1)} custom-call(s32[1]{0:T(128)S(6)} %copy.13.lengths, s32[2]{0:T(128)} %pad_add_fusion.starts, bf16[128,128,128]{2,1,0:T(8,128)(2,1)} %pair.3, f32[1,128]{1,0:T(1,128)} %bitcast.8, f32[1,128]{1,0:T(1,128)} %bitcast.10, bf16[512,128]{1,0:T(8,128)(2,1)} %bitcast.7), custom_call_target="tpu_custom_call" | custom-call | tf_op jit(solution)/shard_map/project/pallas_call | solution.py:217
  16.9 0.0 copy-start.1
  16.9 0.0 copy-start.2
  16.9 278.2 %exchange.1.tri = bf16[128,128,128]{2,1,0:T(8,128)(2,1)S(1)} custom-call(bf16[2,128,128,128]{3,2,1,0:T(8,128)(2,1)} %project.1.send), custom_call_target="tpu_custom_call" | custom-call | tf_op jit(solution)/shard_map/exchange/pallas_call | solution.py:235
  295.1 0.0 copy-start
  295.1 1.9 copy-done
  297.0 0.0 copy-done.1
  297.0 0.7 copy.11.out_gain
  297.7 0.0 copy-done.2
  297.7 0.7 copy.12.out_bias
  298.5 13.8 %finish.1 = bf16[128,128,128]{2,1,0:T(8,128)(2,1)} custom-call(bf16[128,128,128]{2,1,0:T(8,128)(2,1)} %pair.3, bf16[128,128,128]{2,1,0:T(8,128)(2,1)} %copy-done, f32[1,128]{1,0:T(1,128)} %bitcast.9, f32[1,128]{1,0:T(1,128)} %bitcast.11, bf16[128,128]{1,0:T(8,128)(2,1)} %w_gate.1, f32[128,1]{1,0:T(8,128)} %copy.11.out_gain, f32[128,1]{1,0:T(8,128)} %copy.12.out_bias, ...), custom_call_target="tpu_custom_call" | custom-call | tf_op jit(solution)/shard_map/finish/pallas_call | solution.py:254
Async XLA Ops:
  16.9 280.1 %copy-start.1 = (f32[128]{0:T(128)S(1)}, f32[128]{0:T(128)}, u32[]{:S(2)}) copy-start(f32[128]{0:T(128)} %param.15) | copy-start | bytes 1540
  16.9 280.9 %copy-start.2 = (f32[128]{0:T(128)S(1)}, f32[128]{0:T(128)}, u32[]{:S(2)}) copy-start(f32[128]{0:T(128)} %param.16) | copy-start | bytes 1540
  295.1 1.9 copy-start

commit v2 on v1

--- a/solution.py
+++ b/solution.py
@@ -7,7 +7,8 @@
 from jax.experimental.pallas import tpu as pltpu
 from jax.sharding import PartitionSpec as P
 
-CHUNKS = 2
+CHUNKS = 16
+LAG = 2
 ROWS = 16
 
 
@@ -83,102 +84,198 @@
 
 
 def exchange_kernel(
-    ny, nx, nz, send, out, held, tri, in_send, in_recv, out_send, out_recv, own_sem
+    nx,
+    nz,
+    send,
+    out,
+    held,
+    given,
+    taken,
+    tri,
+    deal_send,
+    deal_recv,
+    pass_send,
+    pass_recv,
+    cross_send,
+    cross_recv,
+    back_send,
+    back_recv,
+    own_sem,
 ):
-    n = ny * nx * nz
+    nr = nx * nz
     hidden, rows, cols = send.shape[1:]
-    each = hidden // n
-    part = each // CHUNKS
+    each = hidden // nr
+    chunks = pass_send.shape[0]
+    part = each // chunks
     gy, gx, gz = lax.axis_index("gy"), lax.axis_index("gx"), lax.axis_index("gz")
-    me = (gx * nz + gz) * ny + gy
-
-    def where(index):
-        tall, wide = index // ny, index % ny
-        return (
-            {"gy": wide, "gx": tall // nz, "gz": tall % nz},
-            pl.ds(pl.multiple_of(tall * rows, rows), rows),
-            pl.ds(pl.multiple_of(wide * cols, cols), cols),
-        )
-
-    def deal(chunk, step):
-        peer = lax.rem(me + step, n)
-        _, my_rows, my_cols = where(me)
-        slot = chunk * n + step
+    me = gx * nz + gz
+    half = gy // 2
+    inner_plane, outer_plane = 1 + half, 3 * half
+    inner = gy == inner_plane
+
+    def place(tall, plane):
+        return {"gy": plane, "gx": tall // nz, "gz": tall % nz}
+
+    def remote(src, dst, send_sem, recv_sem, device):
         return pltpu.make_async_remote_copy(
-            src_ref=send.at[:, pl.ds(peer * each + chunk * part, part)],
-            dst_ref=held.at[:, pl.ds(chunk * part, part), my_rows, my_cols],
-            send_sem=in_send.at[slot],
-            recv_sem=in_recv.at[slot],
-            device_id=where(peer)[0],
-            device_id_type=pl.DeviceIdType.MESH,
-        )
-
-    def hand_back(chunk, step):
-        peer = lax.rem(me + step, n)
-        device, its_rows, its_cols = where(peer)
-        slot = chunk * n + step
-        return pltpu.make_async_remote_copy(
-            src_ref=tri.at[pl.ds(chunk * part, part), its_rows, its_cols],
-            dst_ref=out.at[pl.ds(me * each + chunk * part, part)],
-            send_sem=out_send.at[slot],
-            recv_sem=out_recv.at[slot],
+            src_ref=src,
+            dst_ref=dst,
+            send_sem=send_sem,
+            recv_sem=recv_sem,
             device_id=device,
             device_id_type=pl.DeviceIdType.MESH,
         )
 
+    def channels(chunk):
+        return pl.ds(chunk * part, part)
+
+    def band(tall):
+        return pl.ds(pl.multiple_of(tall * rows, rows), rows)
+
+    def columns(plane):
+        return pl.ds(pl.multiple_of((plane - 2 * half) * cols, cols), cols)
+
+    def deal(chunk, step):
+        peer = lax.rem(me + step, nr)
+        return remote(
+            send.at[:, pl.ds(peer * each + chunk * part, part)],
+            held.at[:, channels(chunk), band(me), pl.ds(0, cols)],
+            deal_send.at[chunk, step],
+            deal_recv.at[chunk, step],
+            place(peer, gy),
+        )
+
     def keep_in(chunk):
-        _, my_rows, my_cols = where(me)
         return pltpu.make_async_copy(
             send.at[:, pl.ds(me * each + chunk * part, part)],
-            held.at[:, pl.ds(chunk * part, part), my_rows, my_cols],
-            own_sem.at[chunk],
+            held.at[:, channels(chunk), band(me), pl.ds(0, cols)],
+            own_sem.at[0, chunk],
+        )
+
+    def pass_on(chunk):
+        return remote(
+            held.at[:, channels(chunk), :, pl.ds(0, cols)],
+            held.at[:, channels(chunk), :, pl.ds(cols, cols)],
+            pass_send.at[chunk],
+            pass_recv.at[chunk],
+            place(me, inner_plane),
+        )
+
+    def cross(chunk):
+        return remote(
+            given.at[channels(chunk)],
+            taken.at[channels(chunk)],
+            cross_send.at[chunk],
+            cross_recv.at[chunk],
+            place(me, 3 - gy),
+        )
+
+    def hand_back(chunk, step, plane, side):
+        peer = lax.rem(me + step, nr)
+        return remote(
+            tri.at[channels(chunk), band(peer), columns(plane)],
+            out.at[pl.ds(me * each + chunk * part, part)],
+            back_send.at[side, chunk, step],
+            back_recv.at[chunk, step],
+            place(peer, plane),
         )
 
     def keep_out(chunk):
-        _, my_rows, my_cols = where(me)
         return pltpu.make_async_copy(
-            tri.at[pl.ds(chunk * part, part), my_rows, my_cols],
+            tri.at[channels(chunk), band(me), columns(inner_plane)],
             out.at[pl.ds(me * each + chunk * part, part)],
-            own_sem.at[CHUNKS + chunk],
+            own_sem.at[1, chunk],
         )
 
     barrier = pltpu.get_barrier_semaphore()
-    for step in range(1, n):
+    total = 4 * nr
+    index = gy * nr + me
+    for step in range(1, total):
+        peer = lax.rem(index + step, total)
         pl.semaphore_signal(
             barrier,
             inc=1,
-            device_id=where(lax.rem(me + step, n))[0],
+            device_id=place(peer % nr, peer // nr),
             device_id_type=pl.DeviceIdType.MESH,
         )
-    pl.semaphore_wait(barrier, n - 1)
-
-    for chunk in range(CHUNKS):
-        for step in range(1, n):
+    pl.semaphore_wait(barrier, total - 1)
+
+    @pl.loop(0, chunks)
+    def _(chunk):
+        for step in range(1, nr):
             deal(chunk, step).start()
         keep_in(chunk).start()
-    for chunk in range(CHUNKS):
-        for step in range(1, n):
+
+    def dealt(chunk):
+        for step in range(1, nr):
             deal(chunk, step).wait_recv()
         keep_in(chunk).wait()
 
-        @pl.loop(chunk * part, (chunk + 1) * part)
-        def _(channel):
-            tri[channel] = lax.dot_general(
-                held[0, channel],
-                held[1, channel],
-                (((1,), (1,)), ((), ())),
-                preferred_element_type=jnp.float32,
-            ).astype(jnp.bfloat16)
-
-        for step in range(1, n):
-            hand_back(chunk, step).start()
-        keep_out(chunk).start()
-    for chunk in range(CHUNKS):
-        for step in range(1, n):
-            hand_back(chunk, step).wait_recv()
-            deal(chunk, step).wait_send()
-            hand_back(chunk, step).wait_send()
-        keep_out(chunk).wait()
+    def product(channel, which):
+        below = pl.ds(pl.multiple_of(which * 2 * cols, 2 * cols), 2 * cols)
+        return lax.dot_general(
+            held[0, channel],
+            held[1, channel, below, :],
+            (((1,), (1,)), ((), ())),
+            preferred_element_type=jnp.float32,
+        )
+
+    @pl.when(jnp.logical_not(inner))
+    def _():
+        @pl.loop(0, chunks)
+        def _(chunk):
+            dealt(chunk)
+            pass_on(chunk).start()
+
+        @pl.loop(0, chunks)
+        def _(chunk):
+            for step in range(nr):
+                hand_back(chunk, step, outer_plane, 1).wait_recv()
+            for step in range(1, nr):
+                deal(chunk, step).wait_send()
+            pass_on(chunk).wait_send()
+
+    @pl.when(inner)
+    def _():
+        @pl.loop(0, chunks + LAG)
+        def _(turn):
+            @pl.when(turn < chunks)
+            def _():
+                dealt(turn)
+                pass_on(turn).wait_recv()
+
+                @pl.loop(turn * part, (turn + 1) * part)
+                def _(channel):
+                    given[channel] = product(channel, 1 - half).astype(jnp.bfloat16)
+
+                cross(turn).start()
+
+            @pl.when(turn >= LAG)
+            def _():
+                chunk = turn - LAG
+                cross(chunk).wait_recv()
+
+                @pl.loop(chunk * part, (chunk + 1) * part)
+                def _(channel):
+                    total = product(channel, half) + taken[channel].astype(jnp.float32)
+                    tri[channel] = total.astype(jnp.bfloat16)
+
+                for step in range(nr):
+                    hand_back(chunk, step, outer_plane, 1).start()
+                for step in range(1, nr):
+                    hand_back(chunk, step, inner_plane, 0).start()
+                keep_out(chunk).start()
+
+        @pl.loop(0, chunks)
+        def _(chunk):
+            for step in range(1, nr):
+                hand_back(chunk, step, inner_plane, 0).wait_recv()
+                hand_back(chunk, step, inner_plane, 0).wait_send()
+                deal(chunk, step).wait_send()
+            for step in range(nr):
+                hand_back(chunk, step, outer_plane, 1).wait_send()
+            cross(chunk).wait_send()
+            keep_out(chunk).wait()
 
 
 def finish_kernel(pair, tri, gain, bias, w_gate, out_gain, out_bias, w_out, out):
@@ -205,7 +302,6 @@
 
 def channel_body(sizes, pair, lengths, ln_gain, ln_bias, w_ab, w_gate, out_gain, out_bias, w_out):
     ny, nx, nz = sizes
-    n = ny * nx * nz
     tile_rows, tile_cols, width = pair.shape
     hidden = w_out.shape[0]
     starts = jnp.stack(
@@ -232,23 +328,31 @@
     )(lengths, starts, pair, gain, bias, w_ab.T)
     dma = pltpu.SemaphoreType.DMA
     any_space = pl.BlockSpec(memory_space=pl.ANY)
+    nr = nx * nz
+    each, side = hidden // nr, nr * tile_rows
     triangle = pl.pallas_call(
-        functools.partial(exchange_kernel, ny, nx, nz),
+        functools.partial(exchange_kernel, nx, nz),
         name="exchange",
         out_shape=jax.ShapeDtypeStruct((hidden, tile_rows, tile_cols), jnp.bfloat16),
         in_specs=[any_space],
         out_specs=any_space,
         scratch_shapes=[
-            pltpu.VMEM((2, hidden // n, nx * nz * tile_rows, ny * tile_cols), jnp.bfloat16),
-            pltpu.VMEM((hidden // n, nx * nz * tile_rows, ny * tile_cols), jnp.bfloat16),
-            dma((CHUNKS * n,)),
-            dma((CHUNKS * n,)),
-            dma((CHUNKS * n,)),
-            dma((CHUNKS * n,)),
-            dma((2 * CHUNKS,)),
+            pltpu.VMEM((2, each, side, 2 * tile_cols), jnp.bfloat16),
+            pltpu.VMEM((each, side, 2 * tile_cols), jnp.bfloat16),
+            pltpu.VMEM((each, side, 2 * tile_cols), jnp.bfloat16),
+            pltpu.VMEM((each, side, 2 * tile_cols), jnp.bfloat16),
+            dma((CHUNKS, nr)),
+            dma((CHUNKS, nr)),
+            dma((CHUNKS,)),
+            dma((CHUNKS,)),
+            dma((CHUNKS,)),
+            dma((CHUNKS,)),
+            dma((2, CHUNKS, nr)),
+            dma((CHUNKS, nr)),
+            dma((2, CHUNKS)),
         ],
         compiler_params=pltpu.CompilerParams(
-            collective_id=0, has_side_effects=True, vmem_limit_bytes=48 * 2**20
+            collective_id=0, has_side_effects=True, vmem_limit_bytes=56 * 2**20
         ),
     )(sides)
     return pl.pallas_call(
@@ -273,14 +377,15 @@
 
 def body(sizes, pair, *rest):
     ny, nx, nz = sizes
-    n = ny * nx * nz
     hidden = rest[-1].shape[0]
     tile_rows, tile_cols, _ = pair.shape
     fits = (
-        hidden % (n * CHUNKS) == 0
-        and tile_rows == tile_cols
-        and ny == nx * nz
+        ny == 4
+        and hidden % (nx * nz * CHUNKS) == 0
+        and nx * nz * tile_rows == ny * tile_cols
+        and tile_rows % ROWS == 0
         and tile_cols % 128 == 0
+        and 2 * 5 * hidden * tile_rows * tile_cols * 2 <= 48 * 2**20
     )
     return channel_body(sizes, pair, *rest) if fits else gather_body(pair, *rest)
 

time: 313 us -> 248 us (0.79)
  Pallas kernels: 306 us -> 240 us
    pallas_call x1, Pallas kernels: 278 us -> 212 us  [channel_body(): pl.pallas_call(functools.partial(exchange_kernel, nx, nz), name='exchange...]
where the time goes in v2:
time: 248 us; the launch traced here: 244 us
  Pallas kernels  240 us (97%)
  local copies, waits for them, and re-layouts  3.12 us (1%)
    pallas_call x1, Pallas kernels, channel_body(): pl.pallas_call(functools.partial(exchange_kernel, nx, nz), name='exchange...  212 us
    pallas_call x1, Pallas kernels, channel_body(): pl.pallas_call(project_kernel, name='project', grid=(steps,), out_shape=j...  13.9 us
    pallas_call x1, Pallas kernels, channel_body(): pl.pallas_call(finish_kernel, name='finish', grid=(steps,), out_shape=jax...  13.8 us

profile of v2, /device:TPU:9, one launch (start us, length us, event | category | flops | bytes accessed | tf_op | source)
XLA Modules:
  0.0 244.4 jit_solution(15642498527379902245)
XLA Ops:
  0.0 0.6 pad_add_fusion.starts
  0.6 1.7 copy.10
  2.9 13.9 %project.1.send = bf16[2,128,128,128]{3,2,1,0:T(8,128)(2,1)} custom-call(s32[1]{0:T(128)S(6)} %copy.13.lengths, s32[2]{0:T(128)} %pad_add_fusion.starts, bf16[128,128,128]{2,1,0:T(8,128)(2,1)} %pair.3, f32[1,128]{1,0:T(1,128)} %bitcast.8, f32[1,128]{1,0:T(1,128)} %bitcast.10, bf16[512,128]{1,0:T(8,128)(2,1)} %bitcast.7), custom_call_target="tpu_custom_call" | custom-call | tf_op jit(solution)/shard_map/project/pallas_call | solution.py:313
  16.8 0.0 copy-start
  16.8 0.0 copy-start.1
  16.8 212.3 %exchange.1.tri = bf16[128,128,128]{2,1,0:T(8,128)(2,1)} custom-call(bf16[2,128,128,128]{3,2,1,0:T(8,128)(2,1)} %project.1.send), custom_call_target="tpu_custom_call" | custom-call | tf_op jit(solution)/shard_map/exchange/pallas_call | solution.py:333
  229.2 0.0 copy-done
  229.2 0.7 copy.11.out_gain
  229.9 0.0 copy-done.1
  229.9 0.7 copy.12.out_bias
  230.6 13.8 %finish.1 = bf16[128,128,128]{2,1,0:T(8,128)(2,1)} custom-call(bf16[128,128,128]{2,1,0:T(8,128)(2,1)} %pair.3, bf16[128,128,128]{2,1,0:T(8,128)(2,1)} %exchange.1.tri, f32[1,128]{1,0:T(1,128)} %bitcast.9, f32[1,128]{1,0:T(1,128)} %bitcast.11, bf16[128,128]{1,0:T(8,128)(2,1)} %w_gate.1, f32[128,1]{1,0:T(8,128)} %copy.11.out_gain, f32[128,1]{1,0:T(8,128)} %copy.12.out_bias, ...), custom_call_target="tpu_custom_call" | custom-call | tf_op jit(solution)/shard_map/finish/pallas_call | solution.py:358
Async XLA Ops:
  16.8 212.3 %copy-start = (f32[128]{0:T(128)S(1)}, f32[128]{0:T(128)}, u32[]{:S(2)}) copy-start(f32[128]{0:T(128)} %param.15) | copy-start | bytes 1540
  16.8 213.1 %copy-start.1 = (f32[128]{0:T(128)S(1)}, f32[128]{0:T(128)}, u32[]{:S(2)}) copy-start(f32[128]{0:T(128)} %param.16) | copy-start | bytes 1540

commit v3 on v2

--- a/solution.py
+++ b/solution.py
@@ -7,7 +7,7 @@
 from jax.experimental.pallas import tpu as pltpu
 from jax.sharding import PartitionSpec as P
 
-CHUNKS = 16
+CHUNKS = 32
 LAG = 2
 ROWS = 16
 
@@ -63,17 +63,18 @@
     return (gate * projected).astype(jnp.bfloat16)
 
 
-def project_kernel(lengths, starts, pair, gain, bias, w_t, out):
+def project_kernel(nz, lengths, pair, gain, bias, w_ab, out):
     rows, cols, width = pair.shape
     hidden = out.shape[1]
     flat = pair[...].reshape(rows * cols, width)
     normed = layer_norm(flat, gain[...], bias[...]).astype(jnp.bfloat16)
     proj = lax.dot_general(
-        w_t[...], normed, (((1,), (1,)), ((), ())), preferred_element_type=jnp.float32
+        w_ab[...], normed, (((0,), (1,)), ((), ())), preferred_element_type=jnp.float32
     )
     lane = lax.broadcasted_iota(jnp.int32, (1, rows * cols), 1)
-    row = starts[0] + pl.program_id(0) * rows + lane // cols
-    col = starts[1] + lane % cols
+    block = (lax.axis_index("gx") * nz + lax.axis_index("gz")) * pl.num_programs(0)
+    row = (block + pl.program_id(0)) * rows + lane // cols
+    col = lax.axis_index("gy") * cols + lane % cols
     mask = ((row < lengths[0]) & (col < lengths[0])).astype(jnp.float32)
     for side in range(2):
         base = 2 * side * hidden
@@ -91,7 +92,6 @@
     held,
     given,
     taken,
-    tri,
     deal_send,
     deal_recv,
     pass_send,
@@ -173,7 +173,7 @@
     def hand_back(chunk, step, plane, side):
         peer = lax.rem(me + step, nr)
         return remote(
-            tri.at[channels(chunk), band(peer), columns(plane)],
+            taken.at[channels(chunk), band(peer), columns(plane)],
             out.at[pl.ds(me * each + chunk * part, part)],
             back_send.at[side, chunk, step],
             back_recv.at[chunk, step],
@@ -182,7 +182,7 @@
 
     def keep_out(chunk):
         return pltpu.make_async_copy(
-            tri.at[channels(chunk), band(me), columns(inner_plane)],
+            taken.at[channels(chunk), band(me), columns(inner_plane)],
             out.at[pl.ds(me * each + chunk * part, part)],
             own_sem.at[1, chunk],
         )
@@ -258,7 +258,7 @@
                 @pl.loop(chunk * part, (chunk + 1) * part)
                 def _(channel):
                     total = product(channel, half) + taken[channel].astype(jnp.float32)
-                    tri[channel] = total.astype(jnp.bfloat16)
+                    taken[channel] = total.astype(jnp.bfloat16)
 
                 for step in range(nr):
                     hand_back(chunk, step, outer_plane, 1).start()
@@ -276,6 +276,10 @@
                 hand_back(chunk, step, outer_plane, 1).wait_send()
             cross(chunk).wait_send()
             keep_out(chunk).wait()
+
+
+def upright(row):
+    return jnp.transpose(jnp.broadcast_to(row[...], (row.shape[1], row.shape[1])))[:, :1]
 
 
 def finish_kernel(pair, tri, gain, bias, w_gate, out_gain, out_bias, w_out, out):
@@ -289,7 +293,7 @@
     centred = values - mean
     spread = jnp.mean(jnp.square(centred), 0, keepdims=True)
     scaled = (centred * lax.rsqrt(spread + 1e-05)).reshape(hidden, rows * cols)
-    tri_norm = (scaled * out_gain[...] + out_bias[...]).astype(jnp.bfloat16)
+    tri_norm = (scaled * upright(out_gain) + upright(out_bias)).astype(jnp.bfloat16)
     projected = lax.dot_general(
         tri_norm, w_out[...], (((0,), (0,)), ((), ())), preferred_element_type=jnp.float32
     )
@@ -304,28 +308,24 @@
     ny, nx, nz = sizes
     tile_rows, tile_cols, width = pair.shape
     hidden = w_out.shape[0]
-    starts = jnp.stack(
-        [lax.axis_index(("gx", "gz")) * tile_rows, lax.axis_index("gy") * tile_cols]
-    ).astype(jnp.int32)
     gain, bias = ln_gain[None, :], ln_bias[None, :]
     smem = pl.BlockSpec(memory_space=pltpu.SMEM)
     steps = tile_rows // ROWS
     sides = pl.pallas_call(
-        project_kernel,
+        functools.partial(project_kernel, nz),
         name="project",
         grid=(steps,),
         out_shape=jax.ShapeDtypeStruct((2, hidden, tile_rows, tile_cols), jnp.bfloat16),
         in_specs=[
             smem,
-            smem,
             pl.BlockSpec((ROWS, tile_cols, width), lambda step: (step, 0, 0)),
             whole((1, width)),
             whole((1, width)),
-            whole((4 * hidden, width)),
+            whole((width, 4 * hidden)),
         ],
         out_specs=pl.BlockSpec((2, hidden, ROWS, tile_cols), lambda step: (0, 0, step, 0)),
         compiler_params=pltpu.CompilerParams(vmem_limit_bytes=56 * 2**20),
-    )(lengths, starts, pair, gain, bias, w_ab.T)
+    )(lengths, pair, gain, bias, w_ab)
     dma = pltpu.SemaphoreType.DMA
     any_space = pl.BlockSpec(memory_space=pl.ANY)
     nr = nx * nz
@@ -338,7 +338,6 @@
         out_specs=any_space,
         scratch_shapes=[
             pltpu.VMEM((2, each, side, 2 * tile_cols), jnp.bfloat16),
-            pltpu.VMEM((each, side, 2 * tile_cols), jnp.bfloat16),
             pltpu.VMEM((each, side, 2 * tile_cols), jnp.bfloat16),
             pltpu.VMEM((each, side, 2 * tile_cols), jnp.bfloat16),
             dma((CHUNKS, nr)),
@@ -366,13 +365,13 @@
             whole((1, width)),
             whole((1, width)),
             whole((width, width)),
-            whole((hidden, 1)),
-            whole((hidden, 1)),
+            whole((1, hidden)),
+            whole((1, hidden)),
             whole((hidden, width)),
         ],
         out_specs=pl.BlockSpec((ROWS, tile_cols, width), lambda step: (step, 0, 0)),
         compiler_params=pltpu.CompilerParams(vmem_limit_bytes=56 * 2**20),
-    )(pair, triangle, gain, bias, w_gate, out_gain[:, None], out_bias[:, None], w_out)
+    )(pair, triangle, gain, bias, w_gate, out_gain[None, :], out_bias[None, :], w_out)
 
 
 def body(sizes, pair, *rest):

time: 248 us -> 240 us (0.968)
  Pallas kernels: 240 us -> 236 us
  local copies, waits for them, and re-layouts: 3.12 us -> 0 us
    pallas_call x1, Pallas kernels: 212 us -> 208 us  [channel_body(): pl.pallas_call(functools.partial(exchange_kernel, nx, nz), name='exchange...]
where the time goes in v3:
time: 240 us; the launch traced here: 237 us
  Pallas kernels  236 us (98%)
    pallas_call x1, Pallas kernels, channel_body(): pl.pallas_call(functools.partial(exchange_kernel, nx, nz), name='exchange...  208 us
    pallas_call x1, Pallas kernels, channel_body(): pl.pallas_call(functools.partial(project_kernel, nz), name='project', gri...  14.2 us
    pallas_call x1, Pallas kernels, channel_body(): pl.pallas_call(finish_kernel, name='finish', grid=(steps,), out_shape=jax...  14.1 us

profile of v3, /device:TPU:9, one launch (start us, length us, event | category | flops | bytes accessed | tf_op | source)
XLA Modules:
  0.0 236.8 jit_solution(17153766316371158006)
XLA Ops:
  0.7 14.2 %project.1.send = bf16[2,128,128,128]{3,2,1,0:T(8,128)(2,1)} custom-call(s32[1]{0:T(128)S(6)} %copy.10.lengths, bf16[128,128,128]{2,1,0:T(8,128)(2,1)} %pair.3, f32[1,128]{1,0:T(1,128)} %bitcast.4, f32[1,128]{1,0:T(1,128)} %bitcast.6, bf16[128,512]{1,0:T(8,128)(2,1)} %w_ab.1), custom_call_target="tpu_custom_call" | custom-call | tf_op jit(solution)/shard_map/project/pallas_call | solution.py:314
  14.9 207.8 %exchange.1.tri = bf16[128,128,128]{2,1,0:T(8,128)(2,1)} custom-call(bf16[2,128,128,128]{3,2,1,0:T(8,128)(2,1)} %project.1.send), custom_call_target="tpu_custom_call" | custom-call | tf_op jit(solution)/shard_map/exchange/pallas_call | solution.py:333
  222.7 14.1 %finish.1 = bf16[128,128,128]{2,1,0:T(8,128)(2,1)} custom-call(bf16[128,128,128]{2,1,0:T(8,128)(2,1)} %pair.3, bf16[128,128,128]{2,1,0:T(8,128)(2,1)} %exchange.1.tri, f32[1,128]{1,0:T(1,128)} %bitcast.5, f32[1,128]{1,0:T(1,128)} %bitcast.7, bf16[128,128]{1,0:T(8,128)(2,1)} %w_gate.1, f32[1,128]{1,0:T(1,128)} %bitcast.8, f32[1,128]{1,0:T(1,128)} %bitcast.9, ...), custom_call_target="tpu_custom_call" | custom-call | tf_op jit(solution)/shard_map/finish/pallas_call | solution.py:357

commit v4 on v3

--- a/solution.py
+++ b/solution.py
@@ -8,7 +8,8 @@
 from jax.sharding import PartitionSpec as P
 
 CHUNKS = 32
-LAG = 2
+LAG = 3
+GROUPS = 4
 ROWS = 16
 
 
@@ -63,32 +64,20 @@
     return (gate * projected).astype(jnp.bfloat16)
 
 
-def project_kernel(nz, lengths, pair, gain, bias, w_ab, out):
-    rows, cols, width = pair.shape
-    hidden = out.shape[1]
-    flat = pair[...].reshape(rows * cols, width)
-    normed = layer_norm(flat, gain[...], bias[...]).astype(jnp.bfloat16)
-    proj = lax.dot_general(
-        w_ab[...], normed, (((0,), (1,)), ((), ())), preferred_element_type=jnp.float32
-    )
-    lane = lax.broadcasted_iota(jnp.int32, (1, rows * cols), 1)
-    block = (lax.axis_index("gx") * nz + lax.axis_index("gz")) * pl.num_programs(0)
-    row = (block + pl.program_id(0)) * rows + lane // cols
-    col = lax.axis_index("gy") * cols + lane % cols
-    mask = ((row < lengths[0]) & (col < lengths[0])).astype(jnp.float32)
-    for side in range(2):
-        base = 2 * side * hidden
-        value = (
-            mask * jax.nn.sigmoid(proj[base : base + hidden]) * proj[base + hidden : base + 2 * hidden]
-        )
-        out[side] = value.reshape(hidden, rows, cols).astype(jnp.bfloat16)
-
-
 def exchange_kernel(
     nx,
     nz,
+    lengths,
+    pair,
+    gain,
+    bias,
+    w_ab,
+    w_gate,
+    out,
+    gate_out,
+    normed,
     send,
-    out,
+    gate_held,
     held,
     given,
     taken,
@@ -101,9 +90,13 @@
     back_send,
     back_recv,
     own_sem,
+    pair_sem,
+    gate_sem,
 ):
     nr = nx * nz
     hidden, rows, cols = send.shape[1:]
+    width = pair.shape[2]
+    blocks, lanes = rows // ROWS, ROWS * cols
     each = hidden // nr
     chunks = pass_send.shape[0]
     part = each // chunks
@@ -187,6 +180,15 @@
             own_sem.at[1, chunk],
         )
 
+    def load(block):
+        return pltpu.make_async_copy(
+            pair.at[pl.ds(block * ROWS, ROWS)],
+            normed.at[pl.ds(block * ROWS, ROWS)],
+            pair_sem.at[block],
+        )
+
+    for block in range(blocks):
+        load(block).start()
     barrier = pltpu.get_barrier_semaphore()
     total = 4 * nr
     index = gy * nr + me
@@ -200,12 +202,6 @@
         )
     pl.semaphore_wait(barrier, total - 1)
 
-    @pl.loop(0, chunks)
-    def _(chunk):
-        for step in range(1, nr):
-            deal(chunk, step).start()
-        keep_in(chunk).start()
-
     def dealt(chunk):
         for step in range(1, nr):
             deal(chunk, step).wait_recv()
@@ -220,12 +216,96 @@
             preferred_element_type=jnp.float32,
         )
 
-    @pl.when(jnp.logical_not(inner))
+    @pl.loop(0, blocks)
+    def _(block):
+        load(block).wait()
+        here = pl.ds(pl.multiple_of(block * ROWS, ROWS), ROWS)
+        flat = normed[here].reshape(lanes, width)
+        value = layer_norm(flat, gain[...], bias[...]).astype(jnp.bfloat16)
+        normed[here] = value.reshape(ROWS, cols, width)
+
+    upright_w = jnp.transpose(w_ab[...].astype(jnp.float32))
+    lane = lax.broadcasted_iota(jnp.int32, (1, lanes), 1)
+    col_live = gy * cols + lane % cols < lengths[0]
+    span = each // GROUPS
+
+    def project(group):
+        starts = [
+            kind * hidden + tall * each + group * span for kind in range(4) for tall in range(nr)
+        ]
+        weights = jnp.concatenate([upright_w[at : at + span] for at in starts]).astype(jnp.bfloat16)
+        height = nr * span
+
+        @pl.loop(0, blocks)
+        def _(block):
+            here = pl.ds(pl.multiple_of(block * ROWS, ROWS), ROWS)
+            proj = lax.dot_general(
+                weights,
+                normed[here].reshape(lanes, width),
+                (((1,), (1,)), ((), ())),
+                preferred_element_type=jnp.float32,
+            )
+            row_live = me * rows + block * ROWS + lane // cols < lengths[0]
+            mask = (row_live & col_live).astype(jnp.float32)
+            for side in range(2):
+                gates = proj[2 * side * height : (2 * side + 1) * height]
+                values = proj[(2 * side + 1) * height : (2 * side + 2) * height]
+                value = mask * jax.nn.sigmoid(gates) * values
+                value = value.reshape(height, ROWS, cols).astype(jnp.bfloat16)
+                for tall in range(nr):
+                    first = tall * each + group * span
+                    send[side, first : first + span, here] = value[tall * span : (tall + 1) * span]
+
+        @pl.loop(group * span // part, (group + 1) * span // part)
+        def _(chunk):
+            for step in range(1, nr):
+                deal(chunk, step).start()
+            keep_in(chunk).start()
+
+    outer = jnp.logical_not(inner)
+    for group in range(GROUPS):
+        project(group)
+        if group:
+
+            @pl.when(outer)
+            def _():
+                dealt(group - 1)
+                pass_on(group - 1).start()
+
+    def store_gate(block):
+        return pltpu.make_async_copy(
+            gate_held.at[block % 2],
+            gate_out.at[pl.ds(block * ROWS, ROWS)],
+            gate_sem.at[block % 2],
+        )
+
+    def gate_turn(turn):
+        block = turn - 2 * GROUPS
+
+        @pl.when((block >= 2) & (block < blocks + 2))
+        def _():
+            store_gate(block - 2).wait()
+
+        @pl.when((block >= 0) & (block < blocks))
+        def _():
+            here = pl.ds(pl.multiple_of(block * ROWS, ROWS), ROWS)
+            value = jax.nn.sigmoid(
+                jnp.dot(
+                    normed[here].reshape(lanes, width),
+                    w_gate[...],
+                    preferred_element_type=jnp.float32,
+                )
+            )
+            gate_held[block % 2] = value.reshape(ROWS, cols, width)
+            store_gate(block).start()
+
+    @pl.when(outer)
     def _():
-        @pl.loop(0, chunks)
+        @pl.loop(GROUPS - 1, chunks)
         def _(chunk):
             dealt(chunk)
             pass_on(chunk).start()
+            gate_turn(chunk)
 
         @pl.loop(0, chunks)
         def _(chunk):
@@ -265,6 +345,8 @@
                 for step in range(1, nr):
                     hand_back(chunk, step, inner_plane, 0).start()
                 keep_out(chunk).start()
+
+            gate_turn(turn)
 
         @pl.loop(0, chunks)
         def _(chunk):
@@ -282,12 +364,9 @@
     return jnp.transpose(jnp.broadcast_to(row[...], (row.shape[1], row.shape[1])))[:, :1]
 
 
-def finish_kernel(pair, tri, gain, bias, w_gate, out_gain, out_bias, w_out, out):
-    rows, cols, width = pair.shape
+def finish_kernel(gate, tri, out_gain, out_bias, w_out, out):
+    rows, cols, width = out.shape
     hidden = tri.shape[0]
-    flat = pair[...].reshape(rows * cols, width)
-    normed = layer_norm(flat, gain[...], bias[...]).astype(jnp.bfloat16)
-    gate = jax.nn.sigmoid(jnp.dot(normed, w_gate[...], preferred_element_type=jnp.float32))
     values = tri[...].astype(jnp.float32)
     mean = jnp.mean(values, 0, keepdims=True)
     centred = values - mean
@@ -297,7 +376,7 @@
     projected = lax.dot_general(
         tri_norm, w_out[...], (((0,), (0,)), ((), ())), preferred_element_type=jnp.float32
     )
-    out[...] = (gate * projected).astype(jnp.bfloat16).reshape(rows, cols, width)
+    out[...] = (gate[...] * projected.reshape(rows, cols, width)).astype(jnp.bfloat16)
 
 
 def whole(shape):
@@ -311,32 +390,24 @@
     gain, bias = ln_gain[None, :], ln_bias[None, :]
     smem = pl.BlockSpec(memory_space=pltpu.SMEM)
     steps = tile_rows // ROWS
-    sides = pl.pallas_call(
-        functools.partial(project_kernel, nz),
-        name="project",
-        grid=(steps,),
-        out_shape=jax.ShapeDtypeStruct((2, hidden, tile_rows, tile_cols), jnp.bfloat16),
-        in_specs=[
-            smem,
-            pl.BlockSpec((ROWS, tile_cols, width), lambda step: (step, 0, 0)),
-            whole((1, width)),
-            whole((1, width)),
-            whole((width, 4 * hidden)),
-        ],
-        out_specs=pl.BlockSpec((2, hidden, ROWS, tile_cols), lambda step: (0, 0, step, 0)),
-        compiler_params=pltpu.CompilerParams(vmem_limit_bytes=56 * 2**20),
-    )(lengths, pair, gain, bias, w_ab)
     dma = pltpu.SemaphoreType.DMA
     any_space = pl.BlockSpec(memory_space=pl.ANY)
     nr = nx * nz
     each, side = hidden // nr, nr * tile_rows
-    triangle = pl.pallas_call(
+    vmem = pl.BlockSpec(memory_space=pltpu.VMEM)
+    triangle, gate = pl.pallas_call(
         functools.partial(exchange_kernel, nx, nz),
         name="exchange",
-        out_shape=jax.ShapeDtypeStruct((hidden, tile_rows, tile_cols), jnp.bfloat16),
-        in_specs=[any_space],
-        out_specs=any_space,
+        out_shape=(
+            jax.ShapeDtypeStruct((hidden, tile_rows, tile_cols), jnp.bfloat16),
+            jax.ShapeDtypeStruct(pair.shape, jnp.float32),
+        ),
+        in_specs=[smem, any_space, vmem, vmem, vmem, vmem],
+        out_specs=(any_space, any_space),
         scratch_shapes=[
+            pltpu.VMEM(pair.shape, jnp.bfloat16),
+            pltpu.VMEM((2, hidden, tile_rows, tile_cols), jnp.bfloat16),
+            pltpu.VMEM((2, ROWS, tile_cols, width), jnp.float32),
             pltpu.VMEM((2, each, side, 2 * tile_cols), jnp.bfloat16),
             pltpu.VMEM((each, side, 2 * tile_cols), jnp.bfloat16),
             pltpu.VMEM((each, side, 2 * tile_cols), jnp.bfloat16),
@@ -349,11 +420,13 @@
             dma((2, CHUNKS, nr)),
             dma((CHUNKS, nr)),
             dma((2, CHUNKS)),
+            dma((steps,)),
+            dma((2,)),
         ],
         compiler_params=pltpu.CompilerParams(
-            collective_id=0, has_side_effects=True, vmem_limit_bytes=56 * 2**20
+            collective_id=0, has_side_effects=True, vmem_limit_bytes=63 * 2**20
         ),
-    )(sides)
+    )(lengths, pair, gain, bias, w_ab, w_gate)
     return pl.pallas_call(
         finish_kernel,
         name="finish",
@@ -362,16 +435,13 @@
         in_specs=[
             pl.BlockSpec((ROWS, tile_cols, width), lambda step: (step, 0, 0)),
             pl.BlockSpec((hidden, ROWS, tile_cols), lambda step: (0, step, 0)),
-            whole((1, width)),
-            whole((1, width)),
-            whole((width, width)),
             whole((1, hidden)),
             whole((1, hidden)),
             whole((hidden, width)),
         ],
         out_specs=pl.BlockSpec((ROWS, tile_cols, width), lambda step: (step, 0, 0)),
         compiler_params=pltpu.CompilerParams(vmem_limit_bytes=56 * 2**20),
-    )(pair, triangle, gain, bias, w_gate, out_gain[None, :], out_bias[None, :], w_out)
+    )(gate, triangle, out_gain[None, :], out_bias[None, :], w_out)
 
 
 def body(sizes, pair, *rest):
@@ -381,6 +451,7 @@
     fits = (
         ny == 4
         and hidden % (nx * nz * CHUNKS) == 0
+        and hidden % (nx * nz * GROUPS * 8) == 0
         and nx * nz * tile_rows == ny * tile_cols
         and tile_rows % ROWS == 0
         and tile_cols % 128 == 0

time: 240 us -> 235 us (0.979)
  Pallas kernels: 236 us -> 231 us
    pallas_call x1 -> x0, Pallas kernels: 14.2 us -> none  [channel_body(): pl.pallas_call(functools.partial(project_kernel, nz), name='project', gri...]
    pallas_call x1, Pallas kernels: 208 us -> 219 us  [channel_body(): pl.pallas_call(functools.partial(exchange_kernel, nx, nz), name='exchange...]
where the time goes in v4:
time: 235 us; the launch traced here: 232 us
  Pallas kernels  231 us (98%)
    pallas_call x1, Pallas kernels, channel_body(): pl.pallas_call(functools.partial(exchange_kernel, nx, nz), name='exchange...  219 us
    pallas_call x1, Pallas kernels, channel_body(): pl.pallas_call(finish_kernel, name='finish', grid=(steps,), out_shape=jax...  11.7 us

profile of v4, /device:TPU:9, one launch (start us, length us, event | category | flops | bytes accessed | tf_op | source)
XLA Modules:
  0.0 231.8 jit_solution(8951521629329140273)
XLA Ops:
  0.7 219.3 %exchange.1 = (bf16[128,128,128]{2,1,0:T(8,128)(2,1)}, f32[128,128,128]{2,1,0:T(8,128)}) custom-call(s32[1]{0:T(128)S(6)} %copy.10.lengths, bf16[128,128,128]{2,1,0:T(8,128)(2,1)} %pair.1, f32[1,128]{1,0:T(1,128)} %bitcast.4, f32[1,128]{1,0:T(1,128)} %bitcast.5, bf16[128,512]{1,0:T(8,128)(2,1)} %w_ab.1, bf16[128,128]{1,0:T(8,128)(2,1)} %w_gate.1), custom_call_target="tpu_custom_call" | custom-call | tf_op jit(solution)/shard_map/exchange/pallas_call | solution.py:398
  220.0 11.7 %finish.1 = bf16[128,128,128]{2,1,0:T(8,128)(2,1)} custom-call(f32[128,128,128]{2,1,0:T(8,128)} %get-tuple-element.7.gate, bf16[128,128,128]{2,1,0:T(8,128)(2,1)} %get-tuple-element.8.tri, f32[1,128]{1,0:T(1,128)} %bitcast.6, f32[1,128]{1,0:T(1,128)} %bitcast.7, bf16[128,128]{1,0:T(8,128)(2,1)} %w_out.1), custom_call_target="tpu_custom_call" | custom-call | tf_op jit(solution)/shard_map/finish/pallas_call | solution.py:430

commit v5 on v4

--- a/solution.py
+++ b/solution.py
@@ -8,9 +8,9 @@
 from jax.sharding import PartitionSpec as P
 
 CHUNKS = 32
-LAG = 3
+LAG = 2
 GROUPS = 4
-ROWS = 16
+ROWS = 32
 
 
 def layer_norm(values, gain, bias):
@@ -105,6 +105,7 @@
     half = gy // 2
     inner_plane, outer_plane = 1 + half, 3 * half
     inner = gy == inner_plane
+    outer = jnp.logical_not(inner)
 
     def place(tall, plane):
         return {"gy": plane, "gx": tall // nz, "gz": tall % nz}
@@ -145,13 +146,14 @@
             own_sem.at[0, chunk],
         )
 
-    def pass_on(chunk):
+    def deal_inward(chunk, step):
+        peer = lax.rem(me + step, nr)
         return remote(
-            held.at[:, channels(chunk), :, pl.ds(0, cols)],
-            held.at[:, channels(chunk), :, pl.ds(cols, cols)],
-            pass_send.at[chunk],
-            pass_recv.at[chunk],
-            place(me, inner_plane),
+            send.at[:, pl.ds(peer * each + chunk * part, part)],
+            held.at[:, channels(chunk), band(me), pl.ds(cols, cols)],
+            pass_send.at[chunk, step],
+            pass_recv.at[chunk, step],
+            place(peer, inner_plane),
         )
 
     def cross(chunk):
@@ -200,8 +202,6 @@
             device_id=place(peer % nr, peer // nr),
             device_id_type=pl.DeviceIdType.MESH,
         )
-    pl.semaphore_wait(barrier, total - 1)
-
     def dealt(chunk):
         for step in range(1, nr):
             deal(chunk, step).wait_recv()
@@ -256,21 +256,24 @@
                     first = tall * each + group * span
                     send[side, first : first + span, here] = value[tall * span : (tall + 1) * span]
 
+        if group == 0:
+            pl.semaphore_wait(barrier, total - 1)
+
         @pl.loop(group * span // part, (group + 1) * span // part)
         def _(chunk):
-            for step in range(1, nr):
-                deal(chunk, step).start()
-            keep_in(chunk).start()
-
-    outer = jnp.logical_not(inner)
+            @pl.when(inner)
+            def _():
+                for step in range(1, nr):
+                    deal(chunk, step).start()
+                keep_in(chunk).start()
+
+            @pl.when(outer)
+            def _():
+                for step in range(nr):
+                    deal_inward(chunk, step).start()
+
     for group in range(GROUPS):
         project(group)
-        if group:
-
-            @pl.when(outer)
-            def _():
-                dealt(group - 1)
-                pass_on(group - 1).start()
 
     def store_gate(block):
         return pltpu.make_async_copy(
@@ -301,19 +304,15 @@
 
     @pl.when(outer)
     def _():
-        @pl.loop(GROUPS - 1, chunks)
-        def _(chunk):
-            dealt(chunk)
-            pass_on(chunk).start()
-            gate_turn(chunk)
+        @pl.loop(0, chunks)
+        def _(turn):
+            gate_turn(turn)
 
         @pl.loop(0, chunks)
         def _(chunk):
             for step in range(nr):
                 hand_back(chunk, step, outer_plane, 1).wait_recv()
-            for step in range(1, nr):
-                deal(chunk, step).wait_send()
-            pass_on(chunk).wait_send()
+                deal_inward(chunk, step).wait_send()
 
     @pl.when(inner)
     def _():
@@ -322,7 +321,8 @@
             @pl.when(turn < chunks)
             def _():
                 dealt(turn)
-                pass_on(turn).wait_recv()
+                for step in range(nr):
+                    deal_inward(turn, step).wait_recv()
 
                 @pl.loop(turn * part, (turn + 1) * part)
                 def _(channel):
@@ -413,8 +413,8 @@
             pltpu.VMEM((each, side, 2 * tile_cols), jnp.bfloat16),
             dma((CHUNKS, nr)),
             dma((CHUNKS, nr)),
-            dma((CHUNKS,)),
-            dma((CHUNKS,)),
+            dma((CHUNKS, nr)),
+            dma((CHUNKS, nr)),
             dma((CHUNKS,)),
             dma((CHUNKS,)),
             dma((2, CHUNKS, nr)),

time: 235 us -> 257 us (1.094); the launches traced: 232 us -> 257 us
  Pallas kernels: 231 us -> 256 us
    pallas_call x1, Pallas kernels: 219 us -> 246 us  [channel_body(): pl.pallas_call(functools.partial(exchange_kernel, nx, nz), name='exchange...]
where the time goes in v5:
time: 257 us
  Pallas kernels  256 us (100%)
    pallas_call x1, Pallas kernels, channel_body(): pl.pallas_call(functools.partial(exchange_kernel, nx, nz), name='exchange...  246 us
    pallas_call x1, Pallas kernels, channel_body(): pl.pallas_call(finish_kernel, name='finish', grid=(steps,), out_shape=jax...  10.3 us

profile of v5, /device:TPU:9, one launch (start us, length us, event | category | flops | bytes accessed | tf_op | source)
XLA Modules:
  0.0 256.6 jit_solution(18427345666869589036)
XLA Ops:
  0.7 245.6 %exchange.1 = (bf16[128,128,128]{2,1,0:T(8,128)(2,1)}, f32[128,128,128]{2,1,0:T(8,128)}) custom-call(s32[1]{0:T(128)S(6)} %copy.10.lengths, bf16[128,128,128]{2,1,0:T(8,128)(2,1)} %pair.1, f32[1,128]{1,0:T(1,128)} %bitcast.4, f32[1,128]{1,0:T(1,128)} %bitcast.5, bf16[128,512]{1,0:T(8,128)(2,1)} %w_ab.1, bf16[128,128]{1,0:T(8,128)(2,1)} %w_gate.1), custom_call_target="tpu_custom_call" | custom-call | tf_op jit(solution)/shard_map/exchange/pallas_call | solution.py:398
  246.3 10.3 %finish.1 = bf16[128,128,128]{2,1,0:T(8,128)(2,1)} custom-call(f32[128,128,128]{2,1,0:T(8,128)} %get-tuple-element.7.gate, bf16[128,128,128]{2,1,0:T(8,128)(2,1)} %get-tuple-element.8.tri, f32[1,128]{1,0:T(1,128)} %bitcast.6, f32[1,128]{1,0:T(1,128)} %bitcast.7, bf16[128,128]{1,0:T(8,128)(2,1)} %w_out.1), custom_call_target="tpu_custom_call" | custom-call | tf_op jit(solution)/shard_map/finish/pallas_call | solution.py:430

commit v6 on v4

--- a/solution.py
+++ b/solution.py
@@ -8,9 +8,10 @@
 from jax.sharding import PartitionSpec as P
 
 CHUNKS = 32
-LAG = 3
+LAG = 2
+DIRECT = 2
 GROUPS = 4
-ROWS = 16
+ROWS = 32
 
 
 def layer_norm(values, gain, bias):
@@ -92,6 +93,8 @@
     own_sem,
     pair_sem,
     gate_sem,
+    direct_send,
+    direct_recv,
 ):
     nr = nx * nz
     hidden, rows, cols = send.shape[1:]
@@ -105,6 +108,7 @@
     half = gy // 2
     inner_plane, outer_plane = 1 + half, 3 * half
     inner = gy == inner_plane
+    outer = jnp.logical_not(inner)
 
     def place(tall, plane):
         return {"gy": plane, "gx": tall // nz, "gz": tall % nz}
@@ -152,6 +156,16 @@
             pass_send.at[chunk],
             pass_recv.at[chunk],
             place(me, inner_plane),
+        )
+
+    def deal_inward(chunk, step):
+        peer = lax.rem(me + step, nr)
+        return remote(
+            send.at[:, pl.ds(peer * each + chunk * part, part)],
+            held.at[:, channels(chunk), band(me), pl.ds(cols, cols)],
+            direct_send.at[chunk, step],
+            direct_recv.at[chunk, step],
+            place(peer, inner_plane),
         )
 
     def cross(chunk):
@@ -200,8 +214,6 @@
             device_id=place(peer % nr, peer // nr),
             device_id_type=pl.DeviceIdType.MESH,
         )
-    pl.semaphore_wait(barrier, total - 1)
-
     def dealt(chunk):
         for step in range(1, nr):
             deal(chunk, step).wait_recv()
@@ -256,21 +268,32 @@
                     first = tall * each + group * span
                     send[side, first : first + span, here] = value[tall * span : (tall + 1) * span]
 
+        if group == 0:
+            pl.semaphore_wait(barrier, total - 1)
+
         @pl.loop(group * span // part, (group + 1) * span // part)
         def _(chunk):
-            for step in range(1, nr):
-                deal(chunk, step).start()
-            keep_in(chunk).start()
-
-    outer = jnp.logical_not(inner)
+            direct = outer & (chunk < DIRECT)
+
+            @pl.when(direct)
+            def _():
+                for step in range(nr):
+                    deal_inward(chunk, step).start()
+
+            @pl.when(jnp.logical_not(direct))
+            def _():
+                for step in range(1, nr):
+                    deal(chunk, step).start()
+                keep_in(chunk).start()
+
     for group in range(GROUPS):
         project(group)
         if group:
 
             @pl.when(outer)
             def _():
-                dealt(group - 1)
-                pass_on(group - 1).start()
+                dealt(DIRECT + group - 1)
+                pass_on(DIRECT + group - 1).start()
 
     def store_gate(block):
         return pltpu.make_async_copy(
@@ -301,7 +324,7 @@
 
     @pl.when(outer)
     def _():
-        @pl.loop(GROUPS - 1, chunks)
+        @pl.loop(DIRECT + GROUPS - 1, chunks)
         def _(chunk):
             dealt(chunk)
             pass_on(chunk).start()
@@ -311,9 +334,17 @@
         def _(chunk):
             for step in range(nr):
                 hand_back(chunk, step, outer_plane, 1).wait_recv()
-            for step in range(1, nr):
-                deal(chunk, step).wait_send()
-            pass_on(chunk).wait_send()
+
+            @pl.when(chunk < DIRECT)
+            def _():
+                for step in range(nr):
+                    deal_inward(chunk, step).wait_send()
+
+            @pl.when(chunk >= DIRECT)
+            def _():
+                for step in range(1, nr):
+                    deal(chunk, step).wait_send()
+                pass_on(chunk).wait_send()
 
     @pl.when(inner)
     def _():
@@ -322,7 +353,16 @@
             @pl.when(turn < chunks)
             def _():
                 dealt(turn)
-                pass_on(turn).wait_recv()
+
+                @pl.when(turn < DIRECT)
+                def _():
+                    for step in range(nr):
+                        deal_inward(turn, step).wait_recv()
+
+                @pl.when(turn >= DIRECT)
+                def _():
+                    pass_on(turn).wait_recv()
+
 
                 @pl.loop(turn * part, (turn + 1) * part)
                 def _(channel):
@@ -422,6 +462,8 @@
             dma((2, CHUNKS)),
             dma((steps,)),
             dma((2,)),
+            dma((DIRECT, nr)),
+            dma((DIRECT, nr)),
         ],
         compiler_params=pltpu.CompilerParams(
             collective_id=0, has_side_effects=True, vmem_limit_bytes=63 * 2**20

time: 235 us -> 227 us (0.966)
  Pallas kernels: 231 us -> 223 us
    pallas_call x1, Pallas kernels: 219 us -> 213 us  [channel_body(): pl.pallas_call(functools.partial(exchange_kernel, nx, nz), name='exchange...]
where the time goes in v6:
time: 227 us; the launch traced here: 224 us
  Pallas kernels  223 us (98%)
    pallas_call x1, Pallas kernels, channel_body(): pl.pallas_call(functools.partial(exchange_kernel, nx, nz), name='exchange...  213 us
    pallas_call x1, Pallas kernels, channel_body(): pl.pallas_call(finish_kernel, name='finish', grid=(steps,), out_shape=jax...  10.3 us

profile of v6, /device:TPU:9, one launch (start us, length us, event | category | flops | bytes accessed | tf_op | source)
XLA Modules:
  0.0 223.8 jit_solution(11636215951375854526)
XLA Ops:
  0.7 212.9 %exchange.1 = (bf16[128,128,128]{2,1,0:T(8,128)(2,1)}, f32[128,128,128]{2,1,0:T(8,128)}) custom-call(s32[1]{0:T(128)S(6)} %copy.10.lengths, bf16[128,128,128]{2,1,0:T(8,128)(2,1)} %pair.1, f32[1,128]{1,0:T(1,128)} %bitcast.4, f32[1,128]{1,0:T(1,128)} %bitcast.5, bf16[128,512]{1,0:T(8,128)(2,1)} %w_ab.1, bf16[128,128]{1,0:T(8,128)(2,1)} %w_gate.1), custom_call_target="tpu_custom_call" | custom-call | tf_op jit(solution)/shard_map/exchange/pallas_call | solution.py:438
  213.6 10.3 %finish.1 = bf16[128,128,128]{2,1,0:T(8,128)(2,1)} custom-call(f32[128,128,128]{2,1,0:T(8,128)} %get-tuple-element.7.gate, bf16[128,128,128]{2,1,0:T(8,128)(2,1)} %get-tuple-element.8.tri, f32[1,128]{1,0:T(1,128)} %bitcast.6, f32[1,128]{1,0:T(1,128)} %bitcast.7, bf16[128,128]{1,0:T(8,128)(2,1)} %w_out.1), custom_call_target="tpu_custom_call" | custom-call | tf_op jit(solution)/shard_map/finish/pallas_call | solution.py:472
